TPU v7x, 32 devices: a whole 2x2x4 slice. The times are simulated.
32 devices in a mesh: pair: 8 (over z, x), sector: 4 (over y, core).
Axes of the slice: x: 2, y: 2, z: 4, core: 2. Of those that a mesh axis runs over, the one named last changes fastest.
Arguments:
- wave: bfloat16 [4, 1024, 1024], P('sector', 'pair'), may hold values from -6 to 6
- left_ops: bfloat16 [16, 4, 1024, 1024], P('pair', 'sector'), may hold values from -0.1875 to 0.1875
- right_ops: bfloat16 [16, 4, 1024, 1024], P('pair', 'sector'), may hold values from -0.046875 to 0.046875
- targets: int32 [16, 4], P('pair', 'sector'), may hold values from -1 to 3
- sector_sizes: int32 [4], replicated, may hold values from 256 to 1024
- pair_ids: int32 [16], P('pair'), may hold values from 0 to 15, each once
- pair_coefficients: float32 [16], replicated, may hold values from 0.25 to 2
Outputs:
- sigma_blocks: float32 [4, 1024, 1024], P('sector', 'pair')
Inputs may be any that keep to these rules, and one draw needn't show every extreme that they name: `pair_ids`: each orbital pair once.
All inputs are finite; a program needn't handle non-finite values.
Results may differ from a plain program's by a relative error of at most 0.0029.
Values may be sent and summed in bfloat16 or wider, within the bound.
No kernel may reach another device: no remote copies, remote signals or barrier semaphores. Data moves between devices by JAX's collectives and lax.ppermute only.
A program may use at most 128 MiB of HBM per device.

v0:
```python
import jax
import jax.numpy as jnp
from jax import lax
from jax.sharding import PartitionSpec as P


def body(wave, left_ops, right_ops, targets, sector_sizes, pair_ids, pair_coefficients):
    block = wave.shape[2]
    local_rows = wave.shape[1]
    pair_slots = left_ops.shape[0]
    sectors = sector_sizes.shape[0]
    pair_count = lax.axis_size("pair")
    own_sector = lax.axis_index("sector")
    sector_ids = jnp.arange(sectors, dtype=jnp.int32)
    own_size = jnp.sum(jnp.where(sector_ids == own_sector, sector_sizes, 0))
    col_ids = jnp.arange(block, dtype=jnp.int32)
    row_ids = lax.axis_index("pair") * local_rows + jnp.arange(local_rows, dtype=jnp.int32)
    col_used = col_ids < own_size
    row_used = row_ids < own_size
    masked = wave[0] * (row_used[:, None] & col_used[None, :]).astype(wave.dtype)
    table_ids = jnp.arange(pair_coefficients.shape[0], dtype=jnp.int32)
    factor = jnp.sum(
        jnp.where(pair_ids[:, None] == table_ids[None, :], pair_coefficients[None, :], 0.0), axis=1
    )
    left_mats = left_ops[:, 0]
    right_mats = right_ops[:, 0]
    chosen_targets = targets[:, 0]
    totals = jnp.zeros((sectors, block, block), jnp.float32)
    gathered = lax.all_gather(masked, "pair", axis=0, tiled=True)
    for member in range(pair_slots):
        target = chosen_targets[member]
        left_mat = left_mats[member]
        right_mat = right_mats[member]
        weight = factor[member]

        def present_term(left_mat=left_mat, right_mat=right_mat, weight=weight):
            left = jnp.dot(left_mat, gathered, preferred_element_type=jnp.float32).astype(
                jnp.bfloat16
            )
            term = lax.dot_general(
                left, right_mat, (((1,), (1,)), ((), ())), preferred_element_type=jnp.float32
            )
            return weight * term

        def absent_term():
            return jnp.zeros((block, block), jnp.float32)

        addition = lax.cond(target >= 0, present_term, absent_term)
        place = jnp.maximum(target, 0)
        current = lax.dynamic_index_in_dim(totals, place, 0, keepdims=False)
        totals = lax.dynamic_update_index_in_dim(totals, current + addition, place, 0)
    arranged = totals.reshape(sectors, pair_count, local_rows, block).transpose(1, 0, 2, 3)
    arranged = arranged.reshape(pair_count * sectors * local_rows, block)
    summed = lax.psum_scatter(arranged, ("pair", "sector"), scatter_dimension=0, tiled=True)[None]
    out_mask = (row_used[:, None] & col_used[None, :]).astype(jnp.float32)
    return summed * out_mask[None]


def solution(mesh):
    placed = (
        P("sector", "pair", None),
        P("pair", "sector", None, None),
        P("pair", "sector", None, None),
        P("pair", "sector"),
        P(),
        P("pair"),
        P(),
    )
    return jax.shard_map(
        body, mesh=mesh, in_specs=placed, out_specs=P("sector", "pair", None), check_vma=False
    )
```

profile of v0, /device:TPU:3, one launch (start us, length us, event | category | flops | bytes accessed | tf_op | source)
XLA Modules:
  0.0 304.2 jit_solution(10852317030803112737)
XLA Ops:
  6.5 0.0 all-gather.2.cloned.1.call-start
  6.5 1.3 fusion.22
  7.8 0.6 iota_compare_fusion
  8.5 0.7 add_compare_fusion
  9.1 1.8 and_select_fusion.1
  11.0 0.0 all-gather.2.cloned.1.call-update
  11.0 0.0 reduce-scatter.2.cloned.1.call-start
  11.0 1.3 fusion.23
  14.8 0.9 fusion.21
  15.7 43.0 %all-gather.2.cloned.1.call-done = bf16[1024,1024]{1,0:T(8,128)(2,1)} async-done(((bf16[128,1024]{1,0:T(8,128)(2,1)}), bf16[1024,1024]{1,0:T(8,128)(2,1)}) %all-gather.2.cloned.1.call-update) | async-done | bytes 2097168 | tf_op jit(solution)/shard_map/all_gather | solution.py:29
  58.6 2.5 conditional.2
  58.6 2.5 broadcast_in_dim.32
  61.1 0.0 copy-start.1
  61.1 2.1 broadcast_in_dim.40
  63.3 0.0 copy-done.1
  63.3 0.6 constant_dynamic-update-slice_fusion
  63.9 0.0 copy-start
  63.9 5.7 %copy-done = f32[4,1024,1024]{2,1,0:T(8,128)} copy-done((f32[4,1024,1024]{2,1,0:T(8,128)}, f32[4,1024,1024]{2,1,0:T(8,128)S(1)}, u32[]{:S(2)}) %copy-start) | copy-done | bytes 16777240
  69.7 2.2 constant_dynamic-slice_fusion
  71.9 10.6 %conditional.3 = (f32[1024,1024]{1,0:T(8,128)}) conditional(s32[]{:T(128)} %bitcast.12, () %tuple.21, (f32[2]{0:T(128)S(1)}, bf16[2,1,1024,1024]{3,2,1,0:T(8,128)(2,1)}, bf16[1024,1024]{1,0:T(8,128)(2,1)}, bf16[2,1,1024,1024]{3,2,1,0:T(8,128)(2,1)}) %tuple.20), branch_computations={%region_4.5_spmd, %region_5.6_spmd} | conditional | flops 4297064448 | bytes 10486288 | solution.py:48
  71.9 0.6 slice.31
  72.5 10.0 %convolution_multiply_fusion = f32[1024,1024]{1,0:T(8,128)} fusion(bf16[2,1,1024,1024]{3,2,1,0:T(8,128)(2,1)} %get-tuple-element.47, f32[]{:T(128)} %bitcast.4, bf16[1024,1024]{1,0:T(8,128)(2,1)} %get-tuple-element.46, bf16[2,1,1024,1024]{3,2,1,0:T(8,128)(2,1)} %get-tuple-element.45), kind=kOutput, calls=%fused_computation.7 | convolution fusion | flops 4297064448 | bytes 10486272 | tf_op jit(solution)/shard_map/cond/branch_1_fun/dot_general | solution.py:40
  82.5 6.8 %bitcast_dynamic-update-slice_fusion = f32[4,1024,1024]{2,1,0:T(8,128)} fusion(f32[4,1024,1024]{2,1,0:T(8,128)} %copy-done, s32[]{:T(128)} %bitcast.10, f32[1024,1024]{1,0:T(8,128)} %get-tuple-element.51, f32[1,1024,1024]{2,1,0:T(8,128)} %constant_dynamic-slice_fusion), kind=kLoop, calls=%fused_computation.14 | loop fusion | flops 1048576 | bytes 12583424 | tf_op jit(solution)/shard_map/jit(dynamic_update_index_in_dim)/dynamic_update_slice | solution.py:51
  89.2 11.8 %copy.9 = f32[8,4,128,1024]{3,2,1,0:T(8,128)} copy(f32[8,4,128,1024]{3,2,0,1:T(8,128)} %bitcast.45) | data formatting | bytes 33554432 | tf_op jit(solution)/shard_map/transpose | solution.py:52
  101.0 0.0 reduce-scatter.2.cloned.1.call-update
  101.1 194.3 %reduce-scatter.2.cloned.1.call-done = f32[128,1024]{1,0:T(8,128)} async-done(((f32[4096,1024]{1,0:T(8,128)}), f32[128,1024]{1,0:T(8,128)}) %reduce-scatter.2.cloned.1.call-update) | async-done | bytes 524304 | tf_op jit(solution)/shard_map/reduce_scatter | solution.py:54
  295.4 2.0 fusion.20
Async XLA Ops:
  6.5 52.1 %all-gather.2.cloned.1.call-start = ((), (), s32[]{:S(2)}) async-start(), calls=%async_computation.1 | async-start | bytes 2359296 | tf_op jit(solution)/shard_map/all_gather | solution.py:29
  11.0 284.4 %reduce-scatter.2.cloned.1.call-start = ((), (), s32[]{:S(2)}) async-start(), calls=%async_computation.2 | async-start | bytes 17301504 | tf_op jit(solution)/shard_map/reduce_scatter | solution.py:54
  61.1 2.2 copy-start.1
  63.9 5.7 %copy-start = (f32[4,1024,1024]{2,1,0:T(8,128)}, f32[4,1024,1024]{2,1,0:T(8,128)S(1)}, u32[]{:S(2)}) copy-start(f32[4,1024,1024]{2,1,0:T(8,128)S(1)} %constant_dynamic-update-slice_fusion) | copy-start | bytes 50331652
Sparse Core Ops, SparseCore 0:
  11.1 47.4 all-gather.1
  101.2 194.1 reduce-scatter.1
where the time goes:
time: 305 us; the launch traced here: 304 us
  waiting for transfers between devices  237 us (78%)
  local copies, waits for them, and re-layouts  27 us (9%)
  between operations  15.9 us (5%)
  other arithmetic  14 us (5%)
  matrix products  9.97 us (3%)
    reduce_scatter x1, waiting for transfers between devices, body(): lax.psum_scatter(arranged, ('pair', 'sector'), scatter_dimension=0, tiled...  194 us
    all_gather x1, waiting for transfers between devices, body(): gathered = lax.all_gather(masked, 'pair', axis=0, tiled=True)  43 us
    transpose x1, local copies, waits for them, and re-layouts, body(): totals.reshape(sectors, pair_count, local_rows, block).transpose(1, 0, 2, 3)  11.8 us
    dot_general x1, matrix products, present_term(): lax.dot_general(left, right_mat, (((1,), (1,)), ((), ())), preferred_elem...  9.97 us
    dynamic_update_slice x1, other arithmetic, body(): lax.dynamic_update_index_in_dim(totals, current + addition, place, 0)  6.78 us
  transfers between devices with their start and end apart: 2, of which 2 were waited for; matrix products, arithmetic and copies ran while one was open for 1% of the time, Pallas kernels for 0%

commit v1 on v0

--- a/solution.py
+++ b/solution.py
@@ -26,7 +26,12 @@
     right_mats = right_ops[:, 0]
     chosen_targets = targets[:, 0]
     totals = jnp.zeros((sectors, block, block), jnp.float32)
-    gathered = lax.all_gather(masked, "pair", axis=0, tiled=True)
+    ring = [masked]
+    for hop in range(7):
+        ring.append(lax.ppermute(ring[-1], "pair", [(dev, (dev + 1) % 8) for dev in range(8)]))
+    gathered = jnp.roll(
+        jnp.concatenate(ring[::-1], axis=0), (lax.axis_index("pair") + 1) * ring[0].shape[0], axis=0
+    )
     for member in range(pair_slots):
         target = chosen_targets[member]
         left_mat = left_mats[member]

time: 305 us -> 321 us (1.052)
  waiting for transfers between devices: 237 us -> 248 us
  starting transfers between devices: 0.04 us -> 4.14 us
    ppermute x0 -> x7, waiting for transfers between devices: none -> 47.2 us  [body(): lax.ppermute(ring[-1], 'pair', [(dev, (dev + 1) % 8) for dev in range(8)])]
    all_gather x1 -> x0, waiting for transfers between devices: 43 us -> none  [body(): gathered = lax.all_gather(masked, 'pair', axis=0, tiled=True)]
    reduce_scatter x1, waiting for transfers between devices: 194 us -> 200 us  [body(): lax.psum_scatter(arranged, ('pair', 'sector'), scatter_dimension=0, tiled...]
    ppermute x0 -> x7, starting transfers between devices: none -> 4.14 us  [body(): lax.ppermute(ring[-1], 'pair', [(dev, (dev + 1) % 8) for dev in range(8)])]
  transfers between devices with their start and end apart: 2 -> 8, of which waited for: 2 -> 8; matrix products, arithmetic and copies ran while one was open for 1% -> 1% of each run, Pallas kernels for 0% -> 0%
where the time goes in v1:
time: 321 us; the launch traced here: 320 us
  waiting for transfers between devices  248 us (77%)
  local copies, waits for them, and re-layouts  28.8 us (9%)
  between operations  16.3 us (5%)
  other arithmetic  13.6 us (4%)
  matrix products  9.98 us (3%)
  starting transfers between devices  4.14 us (1%)
    reduce_scatter x1, waiting for transfers between devices, body(): lax.psum_scatter(arranged, ('pair', 'sector'), scatter_dimension=0, tiled...  200 us
    ppermute x7, waiting for transfers between devices, body(): lax.ppermute(ring[-1], 'pair', [(dev, (dev + 1) % 8) for dev in range(8)])  47.2 us
    transpose x1, local copies, waits for them, and re-layouts, body(): totals.reshape(sectors, pair_count, local_rows, block).transpose(1, 0, 2, 3)  11.8 us
    dot_general x1, matrix products, present_term(): lax.dot_general(left, right_mat, (((1,), (1,)), ((), ())), preferred_elem...  9.98 us
    dynamic_update_slice x1, other arithmetic, body(): lax.dynamic_update_index_in_dim(totals, current + addition, place, 0)  6.79 us
  transfers between devices with their start and end apart: 8, of which 8 were waited for; matrix products, arithmetic and copies ran while one was open for 1% of the time, Pallas kernels for 0%

profile of v1, /device:TPU:3, one launch (start us, length us, event | category | flops | bytes accessed | tf_op | source)
XLA Modules:
  0.0 320.3 jit_solution(11338605324247451129)
XLA Ops:
  6.5 0.0 copy-start.2
  6.5 0.0 reduce-scatter.2.cloned.1.call-start
  6.5 1.3 fusion.22
  7.9 0.6 iota_compare_fusion
  8.5 0.7 add_compare_fusion
  9.2 1.1 and_select_fusion.1
  10.3 1.3 collective-permute-start
  11.6 5.9 %collective-permute-done = bf16[128,1024]{1,0:T(8,128)(2,1)S(1)} collective-permute-done((bf16[128,1024]{1,0:T(8,128)(2,1)S(1)}, bf16[128,1024]{1,0:T(8,128)(2,1)S(1)}, u32[]{:S(2)}, u32[]{:S(2)}) %collective-permute-start) | collective-permute-done | bytes 262176 | tf_op jit(solution)/shard_map/ppermute | solution.py:31
  17.5 2.2 collective-permute-start.1
  19.7 6.6 %collective-permute-done.1 = bf16[128,1024]{1,0:T(8,128)(2,1)S(1)} collective-permute-done((bf16[128,1024]{1,0:T(8,128)(2,1)S(1)}, bf16[128,1024]{1,0:T(8,128)(2,1)S(1)}, u32[]{:S(2)}, u32[]{:S(2)}) %collective-permute-start.1) | collective-permute-done | bytes 262176 | tf_op jit(solution)/shard_map/ppermute | solution.py:31
  26.3 0.6 collective-permute-start.2
  26.9 7.8 %collective-permute-done.2 = bf16[128,1024]{1,0:T(8,128)(2,1)S(1)} collective-permute-done((bf16[128,1024]{1,0:T(8,128)(2,1)S(1)}, bf16[128,1024]{1,0:T(8,128)(2,1)S(1)}, u32[]{:S(2)}, u32[]{:S(2)}) %collective-permute-start.2) | collective-permute-done | bytes 262176 | tf_op jit(solution)/shard_map/ppermute | solution.py:31
  34.8 0.0 collective-permute-start.3
  34.8 7.6 %collective-permute-done.3 = bf16[128,1024]{1,0:T(8,128)(2,1)S(1)} collective-permute-done((bf16[128,1024]{1,0:T(8,128)(2,1)S(1)}, bf16[128,1024]{1,0:T(8,128)(2,1)S(1)}, u32[]{:S(2)}, u32[]{:S(2)}) %collective-permute-start.3) | collective-permute-done | bytes 262176 | tf_op jit(solution)/shard_map/ppermute | solution.py:31
  42.4 0.0 collective-permute-start.4
  42.4 7.9 %collective-permute-done.4 = bf16[128,1024]{1,0:T(8,128)(2,1)S(1)} collective-permute-done((bf16[128,1024]{1,0:T(8,128)(2,1)S(1)}, bf16[128,1024]{1,0:T(8,128)(2,1)S(1)}, u32[]{:S(2)}, u32[]{:S(2)}) %collective-permute-start.4) | collective-permute-done | bytes 262176 | tf_op jit(solution)/shard_map/ppermute | solution.py:31
  50.3 0.0 collective-permute-start.5
  50.3 7.9 %collective-permute-done.5 = bf16[128,1024]{1,0:T(8,128)(2,1)S(1)} collective-permute-done((bf16[128,1024]{1,0:T(8,128)(2,1)S(1)}, bf16[128,1024]{1,0:T(8,128)(2,1)S(1)}, u32[]{:S(2)}, u32[]{:S(2)}) %collective-permute-start.5) | collective-permute-done | bytes 262176 | tf_op jit(solution)/shard_map/ppermute | solution.py:31
  58.2 0.0 collective-permute-start.6
  58.2 1.3 fusion.23
  62.2 0.9 fusion.21
  63.1 3.4 %collective-permute-done.6 = bf16[128,1024]{1,0:T(8,128)(2,1)S(1)} collective-permute-done((bf16[128,1024]{1,0:T(8,128)(2,1)S(1)}, bf16[128,1024]{1,0:T(8,128)(2,1)S(1)}, u32[]{:S(2)}, u32[]{:S(2)}) %collective-permute-start.6) | collective-permute-done | bytes 262176 | tf_op jit(solution)/shard_map/ppermute | solution.py:31
  66.7 0.0 copy-done.2
  66.7 0.1 constant_dynamic-update-slice_fusion.8
  67.0 0.1 constant_dynamic-update-slice_fusion
  67.2 1.5 constant_dynamic-slice_fusion.1
  68.7 2.5 conditional.2
  68.7 2.5 broadcast_in_dim.32
  71.2 0.0 copy-start.1
  71.2 2.1 broadcast_in_dim.40
  73.3 0.0 copy-done.1
  73.4 0.6 constant_dynamic-update-slice_fusion.16
  74.0 0.0 copy-start
  74.0 5.7 %copy-done = f32[4,1024,1024]{2,1,0:T(8,128)} copy-done((f32[4,1024,1024]{2,1,0:T(8,128)}, f32[4,1024,1024]{2,1,0:T(8,128)S(1)}, u32[]{:S(2)}) %copy-start) | copy-done | bytes 16777240
  79.8 2.2 constant_dynamic-slice_fusion
  82.0 10.6 %conditional.3 = (f32[1024,1024]{1,0:T(8,128)}) conditional(s32[]{:T(128)} %bitcast.12, () %tuple.21, (f32[2]{0:T(128)S(1)}, bf16[2,1,1024,1024]{3,2,1,0:T(8,128)(2,1)}, bf16[1024,1024]{1,0:T(8,128)(2,1)}, bf16[2,1,1024,1024]{3,2,1,0:T(8,128)(2,1)}) %tuple.20), branch_computations={%region_4.5_spmd, %region_5.6_spmd} | conditional | flops 4297064448 | bytes 10486288 | solution.py:53
  82.0 0.6 slice.31
  82.6 10.0 %convolution_multiply_fusion = f32[1024,1024]{1,0:T(8,128)} fusion(bf16[2,1,1024,1024]{3,2,1,0:T(8,128)(2,1)} %get-tuple-element.47, f32[]{:T(128)} %bitcast.4, bf16[1024,1024]{1,0:T(8,128)(2,1)} %get-tuple-element.46, bf16[2,1,1024,1024]{3,2,1,0:T(8,128)(2,1)} %get-tuple-element.45), kind=kOutput, calls=%fused_computation.7 | convolution fusion | flops 4297064448 | bytes 10486272 | tf_op jit(solution)/shard_map/cond/branch_1_fun/dot_general | solution.py:45
  92.6 6.8 %bitcast_dynamic-update-slice_fusion = f32[4,1024,1024]{2,1,0:T(8,128)} fusion(f32[4,1024,1024]{2,1,0:T(8,128)} %copy-done, s32[]{:T(128)} %bitcast.10, f32[1024,1024]{1,0:T(8,128)} %get-tuple-element.51, f32[1,1024,1024]{2,1,0:T(8,128)} %constant_dynamic-slice_fusion), kind=kLoop, calls=%fused_computation.14 | loop fusion | flops 1048576 | bytes 12583424 | tf_op jit(solution)/shard_map/jit(dynamic_update_index_in_dim)/dynamic_update_slice | solution.py:56
  99.4 11.8 %copy.9 = f32[8,4,128,1024]{3,2,1,0:T(8,128)} copy(f32[8,4,128,1024]{3,2,0,1:T(8,128)} %bitcast.49) | data formatting | bytes 33554432 | tf_op jit(solution)/shard_map/transpose | solution.py:57
  111.2 0.0 reduce-scatter.2.cloned.1.call-update
  111.2 200.4 %reduce-scatter.2.cloned.1.call-done = f32[128,1024]{1,0:T(8,128)} async-done(((f32[4096,1024]{1,0:T(8,128)}), f32[128,1024]{1,0:T(8,128)}) %reduce-scatter.2.cloned.1.call-update) | async-done | bytes 524304 | tf_op jit(solution)/shard_map/reduce_scatter | solution.py:59
  311.5 2.0 fusion.20
  (14 shorter events, 0.3 us)
Async XLA Ops:
  6.5 60.1 %copy-start.2 = (bf16[1,128,1024]{2,1,0:T(8,128)(2,1)S(1)}, bf16[1,128,1024]{2,1,0:T(8,128)(2,1)}, u32[]{:S(2)}) copy-start(bf16[1,128,1024]{2,1,0:T(8,128)(2,1)} %param.11) | copy-start | bytes 786436
  6.5 305.0 %reduce-scatter.2.cloned.1.call-start = ((), (), s32[]{:S(2)}) async-start(), calls=%async_computation.1 | async-start | bytes 17301504 | tf_op jit(solution)/shard_map/reduce_scatter | solution.py:59
  10.3 7.2 %collective-permute-start = (bf16[128,1024]{1,0:T(8,128)(2,1)S(1)}, bf16[128,1024]{1,0:T(8,128)(2,1)S(1)}, u32[]{:S(2)}, u32[]{:S(2)}) collective-permute-start(bf16[128,1024]{1,0:T(8,128)(2,1)S(1)} %and_select_fusion.1), channel_id=1, source_target_pairs={{0,4},{4,8},{8,12},{12,16},{16,20},{20,24},{24,28},{28,0},{1,5},{5... | collective-permute-start | bytes 786440 | tf_op jit(solution)/shard_map/ppermute | solution.py:31
  17.5 8.8 %collective-permute-start.1 = (bf16[128,1024]{1,0:T(8,128)(2,1)S(1)}, bf16[128,1024]{1,0:T(8,128)(2,1)S(1)}, u32[]{:S(2)}, u32[]{:S(2)}) collective-permute-start(bf16[128,1024]{1,0:T(8,128)(2,1)S(1)} %collective-permute-done), channel_id=1, source_target_pairs={{0,4},{4,8},{8,12},{12,16},{16,20},{20,24},{24,28},{28,0},{1,5},{5... | collective-permute-start | bytes 786440 | tf_op jit(solution)/shard_map/ppermute | solution.py:31
  26.3 8.5 %collective-permute-start.2 = (bf16[128,1024]{1,0:T(8,128)(2,1)S(1)}, bf16[128,1024]{1,0:T(8,128)(2,1)S(1)}, u32[]{:S(2)}, u32[]{:S(2)}) collective-permute-start(bf16[128,1024]{1,0:T(8,128)(2,1)S(1)} %collective-permute-done.1), channel_id=1, source_target_pairs={{0,4},{4,8},{8,12},{12,16},{16,20},{20,24},{24,28},{28,0},{1,5},{5... | collective-permute-start | bytes 786440 | tf_op jit(solution)/shard_map/ppermute | solution.py:31
  34.8 7.6 %collective-permute-start.3 = (bf16[128,1024]{1,0:T(8,128)(2,1)S(1)}, bf16[128,1024]{1,0:T(8,128)(2,1)S(1)}, u32[]{:S(2)}, u32[]{:S(2)}) collective-permute-start(bf16[128,1024]{1,0:T(8,128)(2,1)S(1)} %collective-permute-done.2), channel_id=1, source_target_pairs={{0,4},{4,8},{8,12},{12,16},{16,20},{20,24},{24,28},{28,0},{1,5},{5... | collective-permute-start | bytes 786440 | tf_op jit(solution)/shard_map/ppermute | solution.py:31
  42.4 7.9 %collective-permute-start.4 = (bf16[128,1024]{1,0:T(8,128)(2,1)S(1)}, bf16[128,1024]{1,0:T(8,128)(2,1)S(1)}, u32[]{:S(2)}, u32[]{:S(2)}) collective-permute-start(bf16[128,1024]{1,0:T(8,128)(2,1)S(1)} %collective-permute-done.3), channel_id=1, source_target_pairs={{0,4},{4,8},{8,12},{12,16},{16,20},{20,24},{24,28},{28,0},{1,5},{5... | collective-permute-start | bytes 786440 | tf_op jit(solution)/shard_map/ppermute | solution.py:31
  50.3 7.9 %collective-permute-start.5 = (bf16[128,1024]{1,0:T(8,128)(2,1)S(1)}, bf16[128,1024]{1,0:T(8,128)(2,1)S(1)}, u32[]{:S(2)}, u32[]{:S(2)}) collective-permute-start(bf16[128,1024]{1,0:T(8,128)(2,1)S(1)} %collective-permute-done.4), channel_id=1, source_target_pairs={{0,4},{4,8},{8,12},{12,16},{16,20},{20,24},{24,28},{28,0},{1,5},{5... | collective-permute-start | bytes 786440 | tf_op jit(solution)/shard_map/ppermute | solution.py:31
  58.2 8.2 %collective-permute-start.6 = (bf16[128,1024]{1,0:T(8,128)(2,1)S(1)}, bf16[128,1024]{1,0:T(8,128)(2,1)S(1)}, u32[]{:S(2)}, u32[]{:S(2)}) collective-permute-start(bf16[128,1024]{1,0:T(8,128)(2,1)S(1)} %collective-permute-done.5), channel_id=1, source_target_pairs={{0,4},{4,8},{8,12},{12,16},{16,20},{20,24},{24,28},{28,0},{1,5},{5... | collective-permute-start | bytes 786440 | tf_op jit(solution)/shard_map/ppermute | solution.py:31
  71.2 2.2 copy-start.1
  74.0 5.7 %copy-start = (f32[4,1024,1024]{2,1,0:T(8,128)}, f32[4,1024,1024]{2,1,0:T(8,128)S(1)}, u32[]{:S(2)}) copy-start(f32[4,1024,1024]{2,1,0:T(8,128)S(1)} %constant_dynamic-update-slice_fusion.16) | copy-start | bytes 50331652
Sparse Core Ops, SparseCore 0:
  111.3 200.1 reduce-scatter.1
